TPU v7x, 32 devices: a whole 2x2x4 slice. The times are simulated.
32 devices in a mesh: pb: 4 (over y, x), wa: 8 (over z, core).
Axes of the slice: x: 2, y: 2, z: 4, core: 2. Of those that a mesh axis runs over, the one named last changes fastest.
Arguments:
- quartets: int32 [1024, 4, 128], P(('pb', 'wa')), may hold values from -1 to 49151, as said below
- counts: int32 [32], P(('pb', 'wa')), may hold values from 1 to 32, as said below
- eig: bfloat16 [24, 49152], P(None, 'pb'), may hold values from -1.1953125 to 1.1953125
- freq: bfloat16 [49152], P('pb'), may hold values from 0.5 to 2
- phi: bfloat16 [144, 1152], replicated, may hold values from -0.5390625 to 0.5390625
- cells: int32 [8, 9], replicated, may hold values from -2 to 2
Outputs:
- rates: float32 [49152], P(('pb', 'wa'))
Inputs may be any that keep to these rules, and one draw needn't show every extreme that they name: quartets[b, 0, n] is a mode of one of the 1024 q-points of the owner group of slot b (from 0 to 12287); the other three entries are all -1 or all modes of the mesh, and then their q-points and that of the first add up as q1 + q2 = q3 + q4 on the mesh. The used slots of a device are its first counts slots; some device has exactly 32.
All inputs are finite; a program needn't handle non-finite values.
Results may differ from a plain program's by a relative error of at most 0.0023.
Values may be sent and summed in bfloat16 or wider, within the bound.
A program may use at most 64 MiB of HBM per device.

v0:
```python
import math
import jax
import jax.numpy as jnp
from jax import lax
from jax.sharding import PartitionSpec as P

QMESH = 16
smearing = 0.5


def outer_pair(first, second, branches):
    count = first.shape[1]
    first_re = first[:branches][:, None, :]
    first_im = first[branches:][:, None, :]
    second_re = second[:branches][None, :, :]
    second_im = second[branches:][None, :, :]
    real = (first_re * second_re - first_im * second_im).reshape(branches * branches, count)
    imag = (first_re * second_im + first_im * second_re).reshape(branches * branches, count)
    return (real, imag)


def cluster_phase(other_modes, cells, branches):
    points = other_modes // branches
    coords = [points // (QMESH * QMESH), points // QMESH % QMESH, points % QMESH]
    shift = jnp.zeros((cells.shape[0], other_modes.shape[1]), jnp.int32)
    for which in range(3):
        sign = 1 if which == 0 else -1
        for axis_c in range(3):
            shift = (
                shift
                + sign * cells[:, 3 * which + axis_c][:, None] * coords[axis_c][which][None, :]
            )
    angle = jnp.remainder(shift, QMESH).astype(jnp.float32) * (2.0 * math.pi / QMESH)
    return (jnp.cos(angle), jnp.sin(angle))


def occupation(value):
    return 1.0 / (jnp.exp(value) - 1.0)


def contributions(
    first_modes,
    other_modes,
    other_spots,
    valid,
    first_vectors,
    first_freqs,
    vectors,
    frequencies,
    phi,
    cells,
):
    branches = vectors.shape[0] // 2
    count = first_modes.shape[0]
    clusters = cells.shape[0]
    first_vec = jnp.take(first_vectors, first_modes, axis=1).astype(jnp.float32)
    first_freq = jnp.take(first_freqs, first_modes).astype(jnp.float32)
    flat_spots = other_spots.reshape(3 * count)
    gathered = jnp.take(vectors, flat_spots, axis=1).astype(jnp.float32)
    other_freq = jnp.take(frequencies, flat_spots).astype(jnp.float32).reshape(3, count)
    second_vec = gathered[:, :count]
    third_vec = gathered[:, count : 2 * count]
    fourth_vec = gathered[:, 2 * count :]
    far_re, far_im = outer_pair(third_vec, fourth_vec, branches)
    far_im = -far_im
    cosine, sine = cluster_phase(other_modes, cells, branches)
    wide_re = cosine[:, None, :] * far_re[None] - sine[:, None, :] * far_im[None]
    wide_im = cosine[:, None, :] * far_im[None] + sine[:, None, :] * far_re[None]
    wide_re = wide_re.reshape(clusters * branches * branches, count).astype(jnp.bfloat16)
    wide_im = wide_im.reshape(clusters * branches * branches, count).astype(jnp.bfloat16)
    weighted_re = jnp.dot(phi, wide_re, preferred_element_type=jnp.float32)
    weighted_im = jnp.dot(phi, wide_im, preferred_element_type=jnp.float32)
    near_re, near_im = outer_pair(first_vec, second_vec, branches)
    value_re = jnp.sum(near_re * weighted_re - near_im * weighted_im, axis=0)
    value_im = jnp.sum(near_re * weighted_im + near_im * weighted_re, axis=0)
    mismatch = first_freq + other_freq[0] - other_freq[1] - other_freq[2]
    delta = jnp.exp(-((mismatch / smearing) ** 2)) / (smearing * math.sqrt(math.pi))
    weight = (
        (1.0 + occupation(other_freq[0]))
        * occupation(other_freq[1])
        * occupation(other_freq[2])
        / occupation(first_freq)
    )
    product = first_freq * other_freq[0] * other_freq[1] * other_freq[2]
    return jnp.where(
        valid, (value_re * value_re + value_im * value_im) * delta * weight / product, 0.0
    )


def body(quartets, counts, eig, freq, phi, cells):
    local_modes = eig.shape[1]
    workers = lax.axis_size("wa")
    held = quartets.shape[0]
    block = quartets.shape[2]
    group = math.gcd(held, 16)
    table, freq_table = (
        lax.all_gather(eig, "pb", axis=1, tiled=True),
        lax.all_gather(freq, "pb", axis=0, tiled=True),
    )
    per_dest = held // workers
    dealt = quartets.reshape(per_dest, workers, 4, block)
    tallies = jnp.full((1, workers), counts[0], jnp.int32)
    dealt, tallies = (
        lax.all_to_all(dealt, "wa", split_axis=1, concat_axis=1, tiled=True),
        lax.all_to_all(tallies, "wa", split_axis=1, concat_axis=1, tiled=True),
    )
    slot_index = jnp.arange(per_dest, dtype=jnp.int32)[:, None] * workers + lax.axis_index("wa")
    used = (slot_index < tallies).reshape(held)
    pool = dealt.reshape(held, 4, block)
    rank = jnp.cumsum(used.astype(jnp.int32)) - 1
    target = jnp.where(used, rank, held)
    order = (
        jnp.zeros((held,), jnp.int32).at[target].set(jnp.arange(held, dtype=jnp.int32), mode="drop")
    )
    total = jnp.sum(used.astype(jnp.int32))

    def fetch(start):
        picks = lax.dynamic_slice_in_dim(order, start, group, 0)
        return jnp.take(pool, picks, axis=0)

    rounds = (total + group - 1) // group

    def one_round(step, partial_value):
        start = (step * group).astype(jnp.int32)
        blocks = fetch(start)
        live = start + jnp.arange(group, dtype=jnp.int32) < total
        first_modes = blocks[:, 0, :].reshape(group * block)
        others = jnp.transpose(blocks[:, 1:, :], (1, 0, 2)).reshape(3, group * block)
        valid = (others[0] >= 0) & jnp.repeat(live, block)
        clamped = jnp.maximum(others, 0)
        terms = contributions(
            first_modes, clamped, clamped, valid, eig, freq, table, freq_table, phi, cells
        )
        return partial_value.at[first_modes].add(terms)

    partial_value = lax.fori_loop(0, rounds, one_round, jnp.zeros((local_modes,), jnp.float32))
    return lax.psum_scatter(partial_value, "wa", scatter_dimension=0, tiled=True)


def solution(mesh):
    placed = (P(("pb", "wa"), None, None), P(("pb", "wa")), P(None, "pb"), P("pb"), P(), P())
    return jax.shard_map(
        body, mesh=mesh, in_specs=placed, out_specs=P(("pb", "wa")), check_vma=False
    )
```

profile of v0, /device:TPU:4, one launch (start us, length us, event | category | flops | bytes accessed | tf_op | source)
XLA Modules:
  0.0 432.6 jit_solution(528731850995991706)
XLA Ops:
  6.5 3.7 copy.98
  11.6 4.9 %all-to-all-start = ((s32[1,8,1]{2,0,1:T(1,128)}), s32[1,8,1]{2,0,1:T(1,128)S(1)}, u32[]{:S(2)}, u32[]{:S(2)}) async-start(s32[1,8,1]{2,0,1:T(1,128)} %broadcast_in_dim.123), calls=%async_computation | async-start | bytes 8192 | tf_op jit(solution)/shard_map/all_to_all | solution.py:105
  17.8 9.0 %all_gather.7 = bf16[49152]{0:T(1024)(128)(2,1)S(1)} all-gather(bf16[12288]{0:T(1024)(128)(2,1)S(1)} %copy-done), channel_id=1, replica_groups=mesh['pb'=4,'wa'=8] {'pb'}, dimensions={0}, use_global_device_ids=true | all-gather | bytes 122880 | tf_op jit(solution)/shard_map/all_gather | solution.py:98
  27.3 5.1 %all-to-all-start.1 = ((s32[4,8,4,128]{3,2,0,1:T(4,128)}), s32[4,8,4,128]{3,2,0,1:T(4,128)S(1)}, u32[]{:S(2)}, u32[]{:S(2)}) async-start(s32[4,8,4,128]{3,2,0,1:T(4,128)} %copy.94), calls=%async_computation.1 | async-start | bytes 131072 | tf_op jit(solution)/shard_map/all_to_all | solution.py:104
  35.2 3.2 all-to-all-done.1
  38.4 95.9 %all-gather.2.cloned.1.call-done = bf16[24,49152]{0,1:T(8,128)(2,1)} async-done(((bf16[24,12288]{0,1:T(8,128)(2,1)}), bf16[24,49152]{0,1:T(8,128)(2,1)}) %all-gather.2.cloned.1.call-update) | async-done | bytes 2359312 | tf_op jit(solution)/shard_map/all_gather | solution.py:97
  134.3 264.4 %while.13 = (s32[]{:T(128)}, f32[12288]{0:T(1024)S(1)}, s32[]{:T(128)}, s32[32]{0:T(128)S(1)}, s32[32,4,128]{2,1,0:T(4,128)S(1)}, /*index=5*/s32[]{:T(128)}, bf1...) while((s32[]{:T(128)}, f32[12288]{0:T(1024)S(1)}, ...), condition=%wide.region_7.8_spmd, body=%wide.region_3.7_spmd.sunk | while | flops 1385344256 | bytes 61334244 | solution.py:136
  136.3 22.7 %gather_fusion.2 = bf16[6144,24]{1,0:T(8,128)(2,1)S(1)} fusion(bf16[24,49152]{0,1:T(8,128)(2,1)} %get-tuple-element.560, s32[6144]{0:T(1024)S(1)} %broadcast_clamp_fusion.4), kind=kCustom, calls=%fused_computation.2.clone.1 | custom fusion | bytes 614400 | tf_op jit(solution)/shard_map/while/body/jit(_take)/gather | solution.py:59
  160.1 2.5 fusion.55
  171.6 5.2 %subtract_convert_fusion.2 = (bf16[8,144,2048]{2,1,0:T(8,128)(2,1)S(1)}, bf16[8,144,2048]{2,1,0:T(8,128)(2,1)}) fusion(f32[144,2048]{1,0:T(8,128)S(1)} %copy-done.1, f32[8,2048]{1,0:T(8,128)S(1)} %get-tuple-element.513, f32[144,2048]{1,0:T(8,128)} %sub.196, f32[8,2048]{1,0:T(8,128)S(1)} %get-tuple-element.515), kind=kLoop, calls=%fused_computation.8.clone.1 | loop fusion | flops 18874368 | bytes 11927552 | tf_op jit(solution)/shard_map/while/body/convert_element_type | solution.py:69
  181.0 7.9 %gather_fusion.3 = bf16[2048,24]{1,0:T(8,128)(2,1)S(1)} fusion(bf16[24,12288]{0,1:T(8,128)(2,1)} %get-tuple-element.559, s32[2048]{0:T(1024)S(1)} %broadcast_clamp_fusion.5), kind=kCustom, calls=%fused_computation.1.clone.1 | custom fusion | bytes 204800 | tf_op jit(solution)/shard_map/while/body/jit(_take)/gather | solution.py:56
  195.9 4.4 %subtract_reduce_fusion.2 = (f32[2048]{0:T(1024)S(1)}, f32[2048]{0:T(1024)S(1)}) fusion(f32[144,2048]{1,0:T(8,128)} %add.543, f32[144,2048]{1,0:T(8,128)} %sub.195, f32[144,2048]{1,0:T(8,128)S(1)} %copy-done.2, bf16[144,1152]{1,0:T(8,128)(2,1)S(1)} %copy-done.6, bf16[1152,2048]{1,0:T(8,128)(2,1)} %bitcast.164), kind=kOutput, calls=%fused_computation.17.clone.1 | convolution fusion | flops 681832448 | bytes 8605696 | tf_op jit(solution)/shard_map/while/body/dot_general | solution.py:72
  200.4 38.2 %gather_fusion.1 = bf16[6144]{0:T(1024)(128)(2,1)S(1)} fusion(bf16[49152]{0:T(1024)(128)(2,1)S(1)} %get-tuple-element.564, s32[6144]{0:T(1024)S(1)} %broadcast_clamp_fusion.4), kind=kCustom, calls=%fused_computation.4.clone.1 | custom fusion | bytes 49152 | tf_op jit(solution)/shard_map/while/body/jit(_take)/gather | solution.py:60
  238.6 13.1 %gather_fusion.4 = bf16[2048]{0:T(1024)(128)(2,1)S(1)} fusion(bf16[12288]{0:T(1024)(128)(2,1)S(1)} %get-tuple-element.563, s32[2048]{0:T(1024)S(1)} %broadcast_clamp_fusion.5), kind=kCustom, calls=%fused_computation.3.clone.1 | custom fusion | bytes 16384 | tf_op jit(solution)/shard_map/while/body/jit(_take)/gather | solution.py:57
  251.8 14.7 %scatter_fusion = f32[12288]{0:T(1024)S(1)} fusion(f32[12288]{0:T(1024)S(1)} %get-tuple-element.538, s32[2048]{0:T(1024)S(1)} %bitcast.168, f32[2048]{0:T(1024)S(1)} %fusion.61), kind=kCustom, calls=%fused_computation.5.clone.1 | custom fusion | flops 2048 | bytes 32768 | tf_op jit(solution)/shard_map/while/body/scatter-add | solution.py:134
  268.5 22.6 %gather_fusion.2 = bf16[6144,24]{1,0:T(8,128)(2,1)S(1)} fusion(bf16[24,49152]{0,1:T(8,128)(2,1)} %get-tuple-element.560, s32[6144]{0:T(1024)S(1)} %broadcast_clamp_fusion.4), kind=kCustom, calls=%fused_computation.2.clone.1 | custom fusion | bytes 614400 | tf_op jit(solution)/shard_map/while/body/jit(_take)/gather | solution.py:59
  292.3 2.5 fusion.55
  303.8 5.2 %subtract_convert_fusion.2 = (bf16[8,144,2048]{2,1,0:T(8,128)(2,1)S(1)}, bf16[8,144,2048]{2,1,0:T(8,128)(2,1)}) fusion(f32[144,2048]{1,0:T(8,128)S(1)} %copy-done.1, f32[8,2048]{1,0:T(8,128)S(1)} %get-tuple-element.513, f32[144,2048]{1,0:T(8,128)} %sub.196, f32[8,2048]{1,0:T(8,128)S(1)} %get-tuple-element.515), kind=kLoop, calls=%fused_computation.8.clone.1 | loop fusion | flops 18874368 | bytes 11927552 | tf_op jit(solution)/shard_map/while/body/convert_element_type | solution.py:69
  313.1 7.9 %gather_fusion.3 = bf16[2048,24]{1,0:T(8,128)(2,1)S(1)} fusion(bf16[24,12288]{0,1:T(8,128)(2,1)} %get-tuple-element.559, s32[2048]{0:T(1024)S(1)} %broadcast_clamp_fusion.5), kind=kCustom, calls=%fused_computation.1.clone.1 | custom fusion | bytes 204800 | tf_op jit(solution)/shard_map/while/body/jit(_take)/gather | solution.py:56
  328.1 4.4 %subtract_reduce_fusion.2 = (f32[2048]{0:T(1024)S(1)}, f32[2048]{0:T(1024)S(1)}) fusion(f32[144,2048]{1,0:T(8,128)} %add.543, f32[144,2048]{1,0:T(8,128)} %sub.195, f32[144,2048]{1,0:T(8,128)S(1)} %copy-done.2, bf16[144,1152]{1,0:T(8,128)(2,1)S(1)} %copy-done.6, bf16[1152,2048]{1,0:T(8,128)(2,1)} %bitcast.164), kind=kOutput, calls=%fused_computation.17.clone.1 | convolution fusion | flops 681832448 | bytes 8605696 | tf_op jit(solution)/shard_map/while/body/dot_general | solution.py:72
  332.6 38.2 %gather_fusion.1 = bf16[6144]{0:T(1024)(128)(2,1)S(1)} fusion(bf16[49152]{0:T(1024)(128)(2,1)S(1)} %get-tuple-element.564, s32[6144]{0:T(1024)S(1)} %broadcast_clamp_fusion.4), kind=kCustom, calls=%fused_computation.4.clone.1 | custom fusion | bytes 49152 | tf_op jit(solution)/shard_map/while/body/jit(_take)/gather | solution.py:60
  370.8 13.1 %gather_fusion.4 = bf16[2048]{0:T(1024)(128)(2,1)S(1)} fusion(bf16[12288]{0:T(1024)(128)(2,1)S(1)} %get-tuple-element.563, s32[2048]{0:T(1024)S(1)} %broadcast_clamp_fusion.5), kind=kCustom, calls=%fused_computation.3.clone.1 | custom fusion | bytes 16384 | tf_op jit(solution)/shard_map/while/body/jit(_take)/gather | solution.py:57
  384.0 14.7 %scatter_fusion = f32[12288]{0:T(1024)S(1)} fusion(f32[12288]{0:T(1024)S(1)} %get-tuple-element.538, s32[2048]{0:T(1024)S(1)} %bitcast.168, f32[2048]{0:T(1024)S(1)} %fusion.61), kind=kCustom, calls=%fused_computation.5.clone.1 | custom fusion | flops 2048 | bytes 32768 | tf_op jit(solution)/shard_map/while/body/scatter-add | solution.py:134
  398.7 26.3 %all-reduce = f32[12288]{0:T(1024)S(1)} all-reduce(f32[12288]{0:T(1024)S(1)} %get-tuple-element.210), channel_id=2, replica_groups=mesh['pb'=4,'wa'=8] {'wa'}, use_global_device_ids=true, to_apply=%region_8.9.clone | all-reduce | flops 12288 | bytes 98304
  (150 shorter events, 51.4 us)
Async XLA Ops:
  6.5 127.8 %all-gather.2.cloned.1.call-start = ((), (), s32[]{:S(2)}) async-start(), calls=%async_computation.2 | async-start | bytes 15728640 | tf_op jit(solution)/shard_map/all_gather | solution.py:97
  10.3 6.2 %copy-start.9 = (s32[32,4,128]{2,1,0:T(4,128)S(1)}, s32[32,4,128]{2,1,0:T(4,128)}, u32[]{:S(2)}) copy-start(s32[32,4,128]{2,1,0:T(4,128)} %param.8) | copy-start | bytes 196612
  10.3 6.8 %copy-start.13 = (s32[8,9]{1,0:T(8,128)S(1)}, s32[8,9]{1,0:T(8,128)}, u32[]{:S(2)}) copy-start(s32[8,9]{1,0:T(8,128)} %param.13) | copy-start | bytes 868
  10.3 6.9 %copy-start.14 = (u32[32]{0:T(128)S(1)}, u32[32]{0:T(128)}, u32[]{:S(2)}) copy-start(u32[32]{0:T(128)} %constant.294) | copy-start | bytes 388
  10.3 7.5 %copy-start = (bf16[12288]{0:T(1024)(128)(2,1)S(1)}, bf16[12288]{0:T(1024)(128)(2,1)}, u32[]{:S(2)}) copy-start(bf16[12288]{0:T(1024)(128)(2,1)} %param.11) | copy-start | bytes 73732
  11.6 15.7 %all-to-all-start = ((s32[1,8,1]{2,0,1:T(1,128)}), s32[1,8,1]{2,0,1:T(1,128)S(1)}, u32[]{:S(2)}, u32[]{:S(2)}) async-start(s32[1,8,1]{2,0,1:T(1,128)} %broadcast_in_dim.123), calls=%async_computation | async-start | bytes 8192 | tf_op jit(solution)/shard_map/all_to_all | solution.py:105
  27.3 11.0 %all-to-all-start.1 = ((s32[4,8,4,128]{3,2,0,1:T(4,128)}), s32[4,8,4,128]{3,2,0,1:T(4,128)S(1)}, u32[]{:S(2)}, u32[]{:S(2)}) async-start(s32[4,8,4,128]{3,2,0,1:T(4,128)} %copy.94), calls=%async_computation.1 | async-start | bytes 131072 | tf_op jit(solution)/shard_map/all_to_all | solution.py:104
  134.3 2.0 copy-start.11
  134.3 2.0 copy-start.7
  169.8 1.8 copy-start.1
  171.6 5.2 %copy-start.5 = (bf16[144,1152]{1,0:T(8,128)(2,1)S(1)}, bf16[144,1152]{1,0:T(8,128)(2,1)}, u32[]{:S(2)}) copy-start(bf16[144,1152]{1,0:T(8,128)(2,1)} %get-tuple-element.562) | copy-start | bytes 995332 | tf_op jit(solution)/shard_map/while
  176.7 2.0 copy-start.4
  194.2 1.8 copy-start.6
  238.6 13.1 %copy-start.10 = (pred[16]{0:T(512)(128)(4,1)S(1)}, pred[16]{0:T(512)(128)(4,1)}, u32[]{:S(2)}) copy-start(pred[16]{0:T(512)(128)(4,1)} %get-tuple-element.520) | copy-start | bytes 52 | tf_op jit(solution)/shard_map/while
  251.8 14.7 %copy-start.8 = (s32[32,4,128]{2,1,0:T(4,128)S(1)}, s32[32,4,128]{2,1,0:T(4,128)}, u32[]{:S(2)}) copy-start(s32[32,4,128]{2,1,0:T(4,128)} %copy-done.7) | copy-start | bytes 196612 | tf_op jit(solution)/shard_map/while
  251.8 14.7 %copy-start.12 = (s32[32]{0:T(128)S(1)}, s32[32]{0:T(128)}, u32[]{:S(2)}) copy-start(s32[32]{0:T(128)} %copy-done.11) | copy-start | bytes 388 | tf_op jit(solution)/shard_map/while
  266.5 2.0 copy-start.11
  266.5 2.0 copy-start.7
  302.0 1.8 copy-start.1
  303.8 5.2 %copy-start.5 = (bf16[144,1152]{1,0:T(8,128)(2,1)S(1)}, bf16[144,1152]{1,0:T(8,128)(2,1)}, u32[]{:S(2)}) copy-start(bf16[144,1152]{1,0:T(8,128)(2,1)} %get-tuple-element.562) | copy-start | bytes 995332 | tf_op jit(solution)/shard_map/while
  308.9 2.0 copy-start.4
  370.8 13.1 %copy-start.10 = (pred[16]{0:T(512)(128)(4,1)S(1)}, pred[16]{0:T(512)(128)(4,1)}, u32[]{:S(2)}) copy-start(pred[16]{0:T(512)(128)(4,1)} %get-tuple-element.520) | copy-start | bytes 52 | tf_op jit(solution)/shard_map/while
  384.0 14.7 %copy-start.8 = (s32[32,4,128]{2,1,0:T(4,128)S(1)}, s32[32,4,128]{2,1,0:T(4,128)}, u32[]{:S(2)}) copy-start(s32[32,4,128]{2,1,0:T(4,128)} %copy-done.7) | copy-start | bytes 196612 | tf_op jit(solution)/shard_map/while
  384.0 14.7 %copy-start.12 = (s32[32]{0:T(128)S(1)}, s32[32]{0:T(128)}, u32[]{:S(2)}) copy-start(s32[32]{0:T(128)} %copy-done.11) | copy-start | bytes 388 | tf_op jit(solution)/shard_map/while
  (5 other events, 7.6 us)
Sparse Core Ops, SparseCore 0:
  10.4 123.8 all-gather.1
where the time goes:
time: 433 us
  local copies, waits for them, and re-layouts  206 us (48%)
  waiting for transfers between devices  99.1 us (23%)
  other arithmetic  53.5 us (12%)
  blocking collectives  35.3 us (8%)
  between operations  15.4 us (4%)
  matrix products  12.8 us (3%)
  starting transfers between devices  9.98 us (2%)
    all_gather x1, waiting for transfers between devices, body(): lax.all_gather(eig, 'pb', axis=1, tiled=True)  95.9 us
    gather x2, local copies, waits for them, and re-layouts, contributions(): jnp.take(frequencies, flat_spots).astype(jnp.float32).reshape(3, count)  76.4 us
    gather x2, local copies, waits for them, and re-layouts, contributions(): gathered = jnp.take(vectors, flat_spots, axis=1).astype(jnp.float32)  45.3 us
    scatter-add x2, other arithmetic, one_round(): return partial_value.at[first_modes].add(terms)  29.4 us
    unnamed x1, blocking collectives  26.3 us
    gather x2, local copies, waits for them, and re-layouts, contributions(): first_freq = jnp.take(first_freqs, first_modes).astype(jnp.float32)  26.2 us
    gather x2, local copies, waits for them, and re-layouts, contributions(): first_vec = jnp.take(first_vectors, first_modes, axis=1).astype(jnp.float32)  15.8 us
    convert_element_type x2, other arithmetic, contributions(): wide_re.reshape(clusters * branches * branches, count).astype(jnp.bfloat16)  10.3 us
  transfers between devices with their start and end apart: 3, of which 2 were waited for; matrix products, arithmetic and copies ran while one was open for 1% of the time, Pallas kernels for 0%

commit v1 on v0

--- a/solution.py
+++ b/solution.py
@@ -94,7 +94,7 @@
     block = quartets.shape[2]
     group = math.gcd(held, 16)
     table, freq_table = (
-        lax.all_gather(eig, "pb", axis=1, tiled=True),
+        jnp.concatenate(lax.all_gather(eig, "pb"), axis=1),
         lax.all_gather(freq, "pb", axis=0, tiled=True),
     )
     per_dest = held // workers

time: 433 us -> 358 us (0.83)
  waiting for transfers between devices: 99.1 us -> 13.4 us
  local copies, waits for them, and re-layouts: 206 us -> 216 us
    all_gather x1, waiting for transfers between devices: 95.9 us -> 9.55 us  [body(): lax.all_gather(eig, 'pb')]
    all_gather x0 -> x1, local copies, waits for them, and re-layouts: none -> 10.1 us  [body(): lax.all_gather(eig, 'pb')]
  transfers between devices with their start and end apart: 3 -> 3, of which waited for: 2 -> 2; matrix products, arithmetic and copies ran while one was open for 1% -> 2% of each run, Pallas kernels for 0% -> 0%
where the time goes in v1:
time: 358 us; the launch traced here: 357 us
  local copies, waits for them, and re-layouts  216 us (60%)
  other arithmetic  53.6 us (15%)
  blocking collectives  35.3 us (10%)
  between operations  15.4 us (4%)
  waiting for transfers between devices  13.4 us (4%)
  matrix products  12.8 us (4%)
  starting transfers between devices  9.71 us (3%)
    gather x2, local copies, waits for them, and re-layouts, contributions(): jnp.take(frequencies, flat_spots).astype(jnp.float32).reshape(3, count)  76.4 us
    gather x2, local copies, waits for them, and re-layouts, contributions(): gathered = jnp.take(vectors, flat_spots, axis=1).astype(jnp.float32)  45.3 us
    scatter-add x2, other arithmetic, one_round(): return partial_value.at[first_modes].add(terms)  29.4 us
    unnamed x1, blocking collectives  26.3 us
    gather x2, local copies, waits for them, and re-layouts, contributions(): first_freq = jnp.take(first_freqs, first_modes).astype(jnp.float32)  26.2 us
    gather x2, local copies, waits for them, and re-layouts, contributions(): first_vec = jnp.take(first_vectors, first_modes, axis=1).astype(jnp.float32)  15.8 us
    convert_element_type x2, other arithmetic, contributions(): wide_re.reshape(clusters * branches * branches, count).astype(jnp.bfloat16)  10.3 us
    all_gather x1, local copies, waits for them, and re-layouts, body(): lax.all_gather(eig, 'pb')  10.1 us
  transfers between devices with their start and end apart: 3, of which 2 were waited for; matrix products, arithmetic and copies ran while one was open for 2% of the time, Pallas kernels for 0%

profile of v1, /device:TPU:4, one launch (start us, length us, event | category | flops | bytes accessed | tf_op | source)
XLA Modules:
  0.0 356.9 jit_solution(12447963979101739622)
XLA Ops:
  8.5 4.9 %all-to-all-start = ((s32[1,8,1]{2,0,1:T(1,128)}), s32[1,8,1]{2,0,1:T(1,128)S(1)}, u32[]{:S(2)}, u32[]{:S(2)}) async-start(s32[1,8,1]{2,0,1:T(1,128)} %broadcast_in_dim.123), calls=%async_computation | async-start | bytes 8192 | tf_op jit(solution)/shard_map/all_to_all | solution.py:105
  13.4 3.8 %copy.98 = bf16[24,12288]{0,1:T(8,128)(2,1)} copy(bf16[24,12288]{1,0:T(8,128)(2,1)} %param.10) | data formatting | bytes 1179648 | tf_op jit(solution)/shard_map/while | solution.py:136
  18.5 9.0 %all_gather.11 = bf16[49152]{0:T(1024)(128)(2,1)S(1)} all-gather(bf16[12288]{0:T(1024)(128)(2,1)S(1)} %copy-done), channel_id=1, replica_groups=mesh['pb'=4,'wa'=8] {'pb'}, dimensions={0}, use_global_device_ids=true | all-gather | bytes 122880 | tf_op jit(solution)/shard_map/all_gather | solution.py:98
  28.2 4.8 %all-to-all-start.1 = ((s32[4,8,4,128]{3,2,0,1:T(4,128)}), s32[4,8,4,128]{3,2,0,1:T(4,128)S(1)}, u32[]{:S(2)}, u32[]{:S(2)}) async-start(s32[4,8,4,128]{3,2,0,1:T(4,128)} %copy.94), calls=%async_computation.1 | async-start | bytes 131072 | tf_op jit(solution)/shard_map/all_to_all | solution.py:104
  35.8 3.2 all-to-all-done.1
  39.0 9.6 %all-gather.3.cloned.1.call-done = bf16[96,12288]{1,0:T(8,128)(2,1)} async-done(((bf16[24,12288]{1,0:T(8,128)(2,1)}), bf16[96,12288]{1,0:T(8,128)(2,1)}) %all-gather.3.cloned.1.call-update) | async-done | bytes 2359312 | tf_op jit(solution)/shard_map/all_gather | solution.py:97
  48.6 10.1 %copy.96 = bf16[4,24,12288]{1,2,0:T(8,128)(2,1)} copy(bf16[4,24,12288]{2,1,0:T(8,128)(2,1)} %bitcast.172) | data formatting | bytes 4718592 | tf_op jit(solution)/shard_map/all_gather | solution.py:97
  58.6 264.4 %while.13 = (s32[]{:T(128)}, f32[12288]{0:T(1024)S(1)}, s32[]{:T(128)}, s32[32]{0:T(128)S(1)}, s32[32,4,128]{2,1,0:T(4,128)S(1)}, /*index=5*/s32[]{:T(128)}, bf1...) while((s32[]{:T(128)}, f32[12288]{0:T(1024)S(1)}, ...), condition=%wide.region_7.8_spmd, body=%wide.region_3.7_spmd.sunk | while | flops 1385344256 | bytes 61334244 | solution.py:136
  60.6 22.7 %gather_fusion.2 = bf16[6144,24]{1,0:T(8,128)(2,1)S(1)} fusion(bf16[24,49152]{0,1:T(8,128)(2,1)} %get-tuple-element.560, s32[6144]{0:T(1024)S(1)} %broadcast_clamp_fusion.4), kind=kCustom, calls=%fused_computation.2.clone.1 | custom fusion | bytes 614400 | tf_op jit(solution)/shard_map/while/body/jit(_take)/gather | solution.py:59
  84.4 2.5 fusion.55
  95.9 5.2 %subtract_convert_fusion.2 = (bf16[8,144,2048]{2,1,0:T(8,128)(2,1)S(1)}, bf16[8,144,2048]{2,1,0:T(8,128)(2,1)}) fusion(f32[144,2048]{1,0:T(8,128)S(1)} %copy-done.1, f32[8,2048]{1,0:T(8,128)S(1)} %get-tuple-element.513, f32[144,2048]{1,0:T(8,128)} %sub.196, f32[8,2048]{1,0:T(8,128)S(1)} %get-tuple-element.515), kind=kLoop, calls=%fused_computation.8.clone.1 | loop fusion | flops 18874368 | bytes 11927552 | tf_op jit(solution)/shard_map/while/body/convert_element_type | solution.py:69
  105.3 7.9 %gather_fusion.3 = bf16[2048,24]{1,0:T(8,128)(2,1)S(1)} fusion(bf16[24,12288]{0,1:T(8,128)(2,1)} %get-tuple-element.559, s32[2048]{0:T(1024)S(1)} %broadcast_clamp_fusion.5), kind=kCustom, calls=%fused_computation.1.clone.1 | custom fusion | bytes 204800 | tf_op jit(solution)/shard_map/while/body/jit(_take)/gather | solution.py:56
  120.2 4.4 %subtract_reduce_fusion.2 = (f32[2048]{0:T(1024)S(1)}, f32[2048]{0:T(1024)S(1)}) fusion(f32[144,2048]{1,0:T(8,128)} %add.543, f32[144,2048]{1,0:T(8,128)} %sub.195, f32[144,2048]{1,0:T(8,128)S(1)} %copy-done.2, bf16[144,1152]{1,0:T(8,128)(2,1)S(1)} %copy-done.6, bf16[1152,2048]{1,0:T(8,128)(2,1)} %bitcast.168), kind=kOutput, calls=%fused_computation.17.clone.1 | convolution fusion | flops 681832448 | bytes 8605696 | tf_op jit(solution)/shard_map/while/body/dot_general | solution.py:72
  124.7 38.2 %gather_fusion.1 = bf16[6144]{0:T(1024)(128)(2,1)S(1)} fusion(bf16[49152]{0:T(1024)(128)(2,1)S(1)} %get-tuple-element.564, s32[6144]{0:T(1024)S(1)} %broadcast_clamp_fusion.4), kind=kCustom, calls=%fused_computation.4.clone.1 | custom fusion | bytes 49152 | tf_op jit(solution)/shard_map/while/body/jit(_take)/gather | solution.py:60
  162.9 13.1 %gather_fusion.4 = bf16[2048]{0:T(1024)(128)(2,1)S(1)} fusion(bf16[12288]{0:T(1024)(128)(2,1)S(1)} %get-tuple-element.563, s32[2048]{0:T(1024)S(1)} %broadcast_clamp_fusion.5), kind=kCustom, calls=%fused_computation.3.clone.1 | custom fusion | bytes 16384 | tf_op jit(solution)/shard_map/while/body/jit(_take)/gather | solution.py:57
  176.1 14.7 %scatter_fusion = f32[12288]{0:T(1024)S(1)} fusion(f32[12288]{0:T(1024)S(1)} %get-tuple-element.538, s32[2048]{0:T(1024)S(1)} %bitcast.174, f32[2048]{0:T(1024)S(1)} %fusion.61), kind=kCustom, calls=%fused_computation.5.clone.1 | custom fusion | flops 2048 | bytes 32768 | tf_op jit(solution)/shard_map/while/body/scatter-add | solution.py:134
  192.8 22.6 %gather_fusion.2 = bf16[6144,24]{1,0:T(8,128)(2,1)S(1)} fusion(bf16[24,49152]{0,1:T(8,128)(2,1)} %get-tuple-element.560, s32[6144]{0:T(1024)S(1)} %broadcast_clamp_fusion.4), kind=kCustom, calls=%fused_computation.2.clone.1 | custom fusion | bytes 614400 | tf_op jit(solution)/shard_map/while/body/jit(_take)/gather | solution.py:59
  228.1 5.2 %subtract_convert_fusion.2 = (bf16[8,144,2048]{2,1,0:T(8,128)(2,1)S(1)}, bf16[8,144,2048]{2,1,0:T(8,128)(2,1)}) fusion(f32[144,2048]{1,0:T(8,128)S(1)} %copy-done.1, f32[8,2048]{1,0:T(8,128)S(1)} %get-tuple-element.513, f32[144,2048]{1,0:T(8,128)} %sub.196, f32[8,2048]{1,0:T(8,128)S(1)} %get-tuple-element.515), kind=kLoop, calls=%fused_computation.8.clone.1 | loop fusion | flops 18874368 | bytes 11927552 | tf_op jit(solution)/shard_map/while/body/convert_element_type | solution.py:69
  237.5 7.9 %gather_fusion.3 = bf16[2048,24]{1,0:T(8,128)(2,1)S(1)} fusion(bf16[24,12288]{0,1:T(8,128)(2,1)} %get-tuple-element.559, s32[2048]{0:T(1024)S(1)} %broadcast_clamp_fusion.5), kind=kCustom, calls=%fused_computation.1.clone.1 | custom fusion | bytes 204800 | tf_op jit(solution)/shard_map/while/body/jit(_take)/gather | solution.py:56
  252.4 4.4 %subtract_reduce_fusion.2 = (f32[2048]{0:T(1024)S(1)}, f32[2048]{0:T(1024)S(1)}) fusion(f32[144,2048]{1,0:T(8,128)} %add.543, f32[144,2048]{1,0:T(8,128)} %sub.195, f32[144,2048]{1,0:T(8,128)S(1)} %copy-done.2, bf16[144,1152]{1,0:T(8,128)(2,1)S(1)} %copy-done.6, bf16[1152,2048]{1,0:T(8,128)(2,1)} %bitcast.168), kind=kOutput, calls=%fused_computation.17.clone.1 | convolution fusion | flops 681832448 | bytes 8605696 | tf_op jit(solution)/shard_map/while/body/dot_general | solution.py:72
  256.9 38.2 %gather_fusion.1 = bf16[6144]{0:T(1024)(128)(2,1)S(1)} fusion(bf16[49152]{0:T(1024)(128)(2,1)S(1)} %get-tuple-element.564, s32[6144]{0:T(1024)S(1)} %broadcast_clamp_fusion.4), kind=kCustom, calls=%fused_computation.4.clone.1 | custom fusion | bytes 49152 | tf_op jit(solution)/shard_map/while/body/jit(_take)/gather | solution.py:60
  295.1 13.1 %gather_fusion.4 = bf16[2048]{0:T(1024)(128)(2,1)S(1)} fusion(bf16[12288]{0:T(1024)(128)(2,1)S(1)} %get-tuple-element.563, s32[2048]{0:T(1024)S(1)} %broadcast_clamp_fusion.5), kind=kCustom, calls=%fused_computation.3.clone.1 | custom fusion | bytes 16384 | tf_op jit(solution)/shard_map/while/body/jit(_take)/gather | solution.py:57
  308.3 14.7 %scatter_fusion = f32[12288]{0:T(1024)S(1)} fusion(f32[12288]{0:T(1024)S(1)} %get-tuple-element.538, s32[2048]{0:T(1024)S(1)} %bitcast.174, f32[2048]{0:T(1024)S(1)} %fusion.61), kind=kCustom, calls=%fused_computation.5.clone.1 | custom fusion | flops 2048 | bytes 32768 | tf_op jit(solution)/shard_map/while/body/scatter-add | solution.py:134
  323.0 26.3 %all-reduce = f32[12288]{0:T(1024)S(1)} all-reduce(f32[12288]{0:T(1024)S(1)} %get-tuple-element.210), channel_id=3, replica_groups=mesh['pb'=4,'wa'=8] {'wa'}, use_global_device_ids=true, to_apply=%region_8.9.clone | all-reduce | flops 12288 | bytes 98304
  (151 shorter events, 54.6 us)
Async XLA Ops:
  6.5 42.0 %all-gather.3.cloned.1.call-start = ((), (), s32[]{:S(2)}) async-start(), calls=%async_computation.2 | async-start | bytes 2949120 | tf_op jit(solution)/shard_map/all_gather | solution.py:97
  8.5 19.7 %all-to-all-start = ((s32[1,8,1]{2,0,1:T(1,128)}), s32[1,8,1]{2,0,1:T(1,128)S(1)}, u32[]{:S(2)}, u32[]{:S(2)}) async-start(s32[1,8,1]{2,0,1:T(1,128)} %broadcast_in_dim.123), calls=%async_computation | async-start | bytes 8192 | tf_op jit(solution)/shard_map/all_to_all | solution.py:105
  13.4 3.8 %copy-start.9 = (s32[32,4,128]{2,1,0:T(4,128)S(1)}, s32[32,4,128]{2,1,0:T(4,128)}, u32[]{:S(2)}) copy-start(s32[32,4,128]{2,1,0:T(4,128)} %param.8) | copy-start | bytes 196612
  13.4 4.5 %copy-start.13 = (s32[8,9]{1,0:T(8,128)S(1)}, s32[8,9]{1,0:T(8,128)}, u32[]{:S(2)}) copy-start(s32[8,9]{1,0:T(8,128)} %param.13) | copy-start | bytes 868
  13.4 4.5 %copy-start.14 = (u32[32]{0:T(128)S(1)}, u32[32]{0:T(128)}, u32[]{:S(2)}) copy-start(u32[32]{0:T(128)} %constant.294) | copy-start | bytes 388
  13.4 5.1 %copy-start = (bf16[12288]{0:T(1024)(128)(2,1)S(1)}, bf16[12288]{0:T(1024)(128)(2,1)}, u32[]{:S(2)}) copy-start(bf16[12288]{0:T(1024)(128)(2,1)} %param.11) | copy-start | bytes 73732
  28.2 10.7 %all-to-all-start.1 = ((s32[4,8,4,128]{3,2,0,1:T(4,128)}), s32[4,8,4,128]{3,2,0,1:T(4,128)S(1)}, u32[]{:S(2)}, u32[]{:S(2)}) async-start(s32[4,8,4,128]{3,2,0,1:T(4,128)} %copy.94), calls=%async_computation.1 | async-start | bytes 131072 | tf_op jit(solution)/shard_map/all_to_all | solution.py:104
  58.6 2.0 copy-start.7
  94.1 1.8 copy-start.1
  95.9 5.2 %copy-start.5 = (bf16[144,1152]{1,0:T(8,128)(2,1)S(1)}, bf16[144,1152]{1,0:T(8,128)(2,1)}, u32[]{:S(2)}) copy-start(bf16[144,1152]{1,0:T(8,128)(2,1)} %get-tuple-element.562) | copy-start | bytes 995332 | tf_op jit(solution)/shard_map/while
  101.1 2.0 copy-start.4
  118.5 1.7 copy-start.2
  118.5 1.8 copy-start.6
  162.9 13.1 %copy-start.10 = (pred[16]{0:T(512)(128)(4,1)S(1)}, pred[16]{0:T(512)(128)(4,1)}, u32[]{:S(2)}) copy-start(pred[16]{0:T(512)(128)(4,1)} %get-tuple-element.520) | copy-start | bytes 52 | tf_op jit(solution)/shard_map/while
  176.1 14.7 %copy-start.8 = (s32[32,4,128]{2,1,0:T(4,128)S(1)}, s32[32,4,128]{2,1,0:T(4,128)}, u32[]{:S(2)}) copy-start(s32[32,4,128]{2,1,0:T(4,128)} %copy-done.7) | copy-start | bytes 196612 | tf_op jit(solution)/shard_map/while
  176.1 14.7 %copy-start.12 = (s32[32]{0:T(128)S(1)}, s32[32]{0:T(128)}, u32[]{:S(2)}) copy-start(s32[32]{0:T(128)} %copy-done.11) | copy-start | bytes 388 | tf_op jit(solution)/shard_map/while
  190.8 2.0 copy-start.7
  226.3 1.8 copy-start.1
  228.1 5.2 %copy-start.5 = (bf16[144,1152]{1,0:T(8,128)(2,1)S(1)}, bf16[144,1152]{1,0:T(8,128)(2,1)}, u32[]{:S(2)}) copy-start(bf16[144,1152]{1,0:T(8,128)(2,1)} %get-tuple-element.562) | copy-start | bytes 995332 | tf_op jit(solution)/shard_map/while
  233.3 2.0 copy-start.4
  250.7 1.8 copy-start.6
  295.1 13.1 %copy-start.10 = (pred[16]{0:T(512)(128)(4,1)S(1)}, pred[16]{0:T(512)(128)(4,1)}, u32[]{:S(2)}) copy-start(pred[16]{0:T(512)(128)(4,1)} %get-tuple-element.520) | copy-start | bytes 52 | tf_op jit(solution)/shard_map/while
  308.3 14.7 %copy-start.8 = (s32[32,4,128]{2,1,0:T(4,128)S(1)}, s32[32,4,128]{2,1,0:T(4,128)}, u32[]{:S(2)}) copy-start(s32[32,4,128]{2,1,0:T(4,128)} %copy-done.7) | copy-start | bytes 196612 | tf_op jit(solution)/shard_map/while
  308.3 14.7 %copy-start.12 = (s32[32]{0:T(128)S(1)}, s32[32]{0:T(128)}, u32[]{:S(2)}) copy-start(s32[32]{0:T(128)} %copy-done.11) | copy-start | bytes 388 | tf_op jit(solution)/shard_map/while
  (5 other events, 6.7 us)
Sparse Core Ops, SparseCore 0:
  9.2 39.3 all-gather.2
